TPU v7x, 32 devices: a whole 2x2x4 slice. The times are simulated.
32 devices in a mesh: leaf: 4 (over x, core), ctx: 8 (over z, y).
Axes of the slice: x: 2, y: 2, z: 4, core: 2. Of those that a mesh axis runs over, the one named last changes fastest.
Arguments:
- queries: bfloat16 [4096, 4096], P(('leaf', 'ctx')), parts along dimension 0, may hold values from -6 to 6
- keys: bfloat16 [4096, 512], P(('leaf', 'ctx')), parts along dimension 0, may hold values from -6 to 6
- values: bfloat16 [4096, 512], P(('leaf', 'ctx')), parts along dimension 0, may hold values from -6 to 6
- grad_out: bfloat16 [4096, 4096], P(('leaf', 'ctx')), parts along dimension 0, may hold values from -6 to 6
- block_path: int32 [32, 4], P('leaf'), parts along dimension 0, may hold values from -1 to 7, as said below
- assistant: int32 [4096], P(('leaf', 'ctx')), parts along dimension 0, may hold values from 0 to 1, as said below
Outputs:
- attention: bfloat16 [4096, 4096], P(('leaf', 'ctx')), parts along dimension 0
- grad_queries: bfloat16 [4096, 4096], P(('leaf', 'ctx')), parts along dimension 0
- grad_keys: bfloat16 [4096, 512], P(('leaf', 'ctx')), parts along dimension 0
- grad_values: bfloat16 [4096, 512], P(('leaf', 'ctx')), parts along dimension 0
There are 4 independent parts, one for each index of `leaf`. A program takes and returns all parts, laid end to end along the dimension named above; each array names one. Nothing has to cross between parts.
Inputs may be any that keep to these rules, and one draw needn't show every extreme that they name: `block_path`: blocks lie in depth-first order of the tree; every node spans one block; block 0 is the root at depth 0. Row b holds at depth e <= depth(b) the block of b's ancestor node at that depth (b itself at e = depth(b)) and -1 below. `assistant`: each block of 128 tokens holds one run of ones.
All inputs are finite; a program needn't handle non-finite values.
Results may differ from a plain program's by a relative error of at most 0.0091.
Values may be sent and summed in bfloat16 or wider, within the bound.
No kernel may reach another device: no remote copies, remote signals or barrier semaphores. Data moves between devices by JAX's collectives and lax.ppermute only.
A program may use at most 128 MiB of HBM per device.

v0:
```python
import math
import jax
import jax.numpy as jnp
from jax import lax
from jax.sharding import PartitionSpec as P

KEY_HEADS = 4
HEAD_WIDTH = 128
HEADS_PER_KEY = 8


def prefix(x, axis, combine, identity):
    size, here = (lax.axis_size(axis), lax.axis_index(axis))
    everything = jax.tree.map(lambda part: lax.all_gather(part, axis), x)
    start = jax.tree.map(
        lambda part, zero: jnp.broadcast_to(jnp.asarray(zero, part.dtype), part.shape), x, identity
    )

    def hop(k, before):
        at = size - 1 - k
        reached = at > here
        new = combine(before, jax.tree.map(lambda part: part[at], everything))
        return jax.tree.map(lambda a, b: jnp.where(reached, a, b), new, before)

    return lax.fori_loop(0, size, hop, start)


def dot_rows(left, right):
    return lax.dot_general(
        left, right, (((1,), (1,)), ((), ())), preferred_element_type=jnp.float32
    )


def dot_cols(left, right):
    return lax.dot_general(
        left, right, (((0,), (0,)), ((), ())), preferred_element_type=jnp.float32
    )


def attend_block(queries, grad_rows, slot_keys, slot_values, allowed):
    block_rows = queries.shape[0]
    head_cols = HEADS_PER_KEY * HEAD_WIDTH
    scaling = 1.0 / math.sqrt(HEAD_WIDTH)
    wide_mask = jnp.repeat(allowed, HEADS_PER_KEY, axis=0)
    attended_parts, query_parts, key_parts, value_parts = ([], [], [], [])
    for key_value_head in range(KEY_HEADS):
        query_matrix = queries[
            :, key_value_head * head_cols : (key_value_head + 1) * head_cols
        ].reshape(block_rows * HEADS_PER_KEY, HEAD_WIDTH)
        grad_head = grad_rows[
            :, key_value_head * head_cols : (key_value_head + 1) * head_cols
        ].reshape(block_rows * HEADS_PER_KEY, HEAD_WIDTH)
        key_cols = slot_keys[:, key_value_head * HEAD_WIDTH : (key_value_head + 1) * HEAD_WIDTH]
        value_cols = slot_values[:, key_value_head * HEAD_WIDTH : (key_value_head + 1) * HEAD_WIDTH]
        scores = jnp.where(wide_mask, dot_rows(query_matrix, key_cols) * scaling, -jnp.inf)
        row_max = jnp.max(scores, axis=1, keepdims=True)
        row_sum = jnp.sum(jnp.exp(scores - row_max), axis=1, keepdims=True)
        log_total = row_max + jnp.log(row_sum)
        rounded = jnp.exp(scores - log_total).astype(jnp.bfloat16)
        attended = jnp.dot(rounded, value_cols, preferred_element_type=jnp.float32).astype(
            jnp.bfloat16
        )
        attended = lax.optimization_barrier(attended)
        row_delta = jnp.sum(
            grad_head.astype(jnp.float32) * attended.astype(jnp.float32), axis=1, keepdims=True
        )
        grad_prob = dot_rows(grad_head, value_cols)
        grad_score = (jnp.exp(scores - log_total) * (grad_prob - row_delta)).astype(jnp.bfloat16)
        grad_query = (
            jnp.dot(grad_score, key_cols, preferred_element_type=jnp.float32) * scaling
        ).astype(jnp.bfloat16)
        grad_key = dot_cols(grad_score, query_matrix) * scaling
        grad_value = dot_cols(rounded, grad_head)
        attended_parts.append(attended.reshape(block_rows, head_cols))
        query_parts.append(grad_query.reshape(block_rows, head_cols))
        key_parts.append(grad_key)
        value_parts.append(grad_value)
    return (
        jnp.concatenate(attended_parts, 1),
        jnp.concatenate(query_parts, 1),
        jnp.concatenate(key_parts, 1),
        jnp.concatenate(value_parts, 1),
    )


def on_device(queries, keys, values, grad_out, block_path, assistant):
    block_rows = queries.shape[0]
    kv_width = keys.shape[1]
    position = lax.axis_index("ctx")
    depths = jnp.sum((block_path >= 0).astype(jnp.int32), axis=1) - 1
    own_path = lax.dynamic_index_in_dim(block_path, position, 0, keepdims=False)
    own_depth = lax.dynamic_index_in_dim(depths, position, 0, keepdims=False)
    seen_slots = jnp.stack([own_depth > 0, own_depth > 1, own_depth > 2])
    wanted_blocks = jnp.stack([own_path[0], own_path[1], own_path[2]])
    row_ids = jnp.arange(block_rows, dtype=jnp.int32)
    empty = jnp.zeros((3, block_rows, kv_width), jnp.bfloat16)
    picked = (empty, empty)
    key_piece = lax.all_gather(keys, "ctx", axis=0, tiled=True)
    value_piece = lax.all_gather(values, "ctx", axis=0, tiled=True)
    piece_rows = key_piece.shape[0]
    for slot_number in range(3):
        wanted = wanted_blocks[slot_number]
        begin = wanted * block_rows
        touches = (wanted >= 0) & (begin < piece_rows) & (begin + block_rows > 0)

        def fill(current, slot_number=slot_number, begin=begin):
            local_rows = begin + row_ids
            inside = (local_rows >= 0) & (local_rows < piece_rows)
            clipped = jnp.clip(local_rows, 0, piece_rows - 1)
            new_keys = jnp.where(inside[:, None], key_piece[clipped], current[0][slot_number])
            new_values = jnp.where(inside[:, None], value_piece[clipped], current[1][slot_number])
            return (
                current[0].at[slot_number].set(new_keys),
                current[1].at[slot_number].set(new_values),
            )

        def unchanged(current):
            return current

        picked = lax.cond(touches, fill, unchanged, picked)
    far_keys, far_values = picked
    slot_keys = jnp.concatenate([far_keys.reshape(3 * block_rows, kv_width), keys], 0)
    slot_values = jnp.concatenate([far_values.reshape(3 * block_rows, kv_width), values], 0)
    full_slots = jnp.repeat(seen_slots, block_rows)
    causal = jnp.arange(block_rows)[:, None] >= jnp.arange(block_rows)[None, :]
    allowed = jnp.concatenate(
        [jnp.broadcast_to(full_slots[None, :], (block_rows, 3 * block_rows)), causal], 1
    )
    grad_rows = grad_out * assistant[:, None].astype(jnp.bfloat16)
    attention, grad_queries, grad_key_all, grad_value_all = attend_block(
        queries, grad_rows, slot_keys, slot_values, allowed
    )
    slot_grads = jnp.stack(
        [
            grad_key_all.reshape(4, block_rows, kv_width),
            grad_value_all.reshape(4, block_rows, kv_width),
        ],
        1,
    )
    grad_total = slot_grads[3]
    tree_depths = [0, 1, 2]
    resets = jnp.stack([own_depth <= tree_level for tree_level in tree_depths]).astype(jnp.float32)
    carried = jnp.stack([slot_grads[tree_level] for tree_level in tree_depths])

    def accumulate(earlier, latter):
        marker = jnp.maximum(earlier[0], latter[0])
        summed = jnp.where(latter[0][:, None, None, None] > 0.5, latter[1], earlier[1] + latter[1])
        return (marker, summed)

    identity = (jnp.zeros_like(resets), jnp.zeros_like(carried))
    _, received = prefix((resets, carried), "ctx", accumulate, identity)
    for slot_index, tree_level in enumerate(tree_depths):
        grad_total = grad_total + jnp.where(own_depth == tree_level, received[slot_index], 0.0)
    return (
        attention,
        grad_queries,
        grad_total[0].astype(jnp.bfloat16),
        grad_total[1].astype(jnp.bfloat16),
    )


def solution(mesh):
    in_specs = (
        P(("leaf", "ctx"), None),
        P(("leaf", "ctx"), None),
        P(("leaf", "ctx"), None),
        P(("leaf", "ctx"), None),
        P("leaf", None),
        P(("leaf", "ctx")),
    )
    out_specs = (
        P(("leaf", "ctx"), None),
        P(("leaf", "ctx"), None),
        P(("leaf", "ctx"), None),
        P(("leaf", "ctx"), None),
    )
    return jax.shard_map(
        on_device, mesh=mesh, in_specs=in_specs, out_specs=out_specs, check_vma=False
    )
```

profile of v0, /device:TPU:0, one launch (start us, length us, event | category | flops | bytes accessed | tf_op | source)
XLA Modules:
  0.0 329.6 jit_solution(16792930033362038903)
XLA Ops:
  23.4 29.8 %all-gather.6.cloned.1.call-done = bf16[1024,512]{1,0:T(8,128)(2,1)} async-done(((bf16[128,512]{1,0:T(8,128)(2,1)}), bf16[1024,512]{1,0:T(8,128)(2,1)}) %all-gather.6.cloned.1.call-update) | async-done | bytes 1048592 | tf_op jit(solution)/shard_map/all_gather | solution.py:98
  53.2 41.1 %all-gather.8.cloned.1.call-done = bf16[1024,512]{1,0:T(8,128)(2,1)} async-done(((bf16[128,512]{1,0:T(8,128)(2,1)}), bf16[1024,512]{1,0:T(8,128)(2,1)}) %all-gather.8.cloned.1.call-update) | async-done | bytes 1048592 | tf_op jit(solution)/shard_map/all_gather | solution.py:99
  94.3 4.7 %conditional.3 = (bf16[3,128,512]{2,1,0:T(8,128)(2,1)S(1)}, bf16[3,128,512]{2,1,0:T(8,128)(2,1)S(1)}) conditional(s32[]{:T(128)} %convert_element_type.109, () %tuple.88, (s32[]{:T(128)}, s32[128]{0:T(128)S(1)}, bf16[1024,512]{1,0:T(8,128)(2,1)}, bf16[1024,512]{1,0:T(8,128)(2,1)}) %tuple.89), branch_computations={%region_1.2_spmd, %region_2.3_spmd} | conditional | flops 133248 | bytes 2104604 | solution.py:120
  94.3 2.2 gather_fusion.1
  96.6 2.2 gather_fusion
  122.8 24.4 %all-gather.1 = f32[8,1,3]{2,1,0:T(1,128)S(1)} all-gather(f32[1,1,3]{2,1,0:T(1,128)S(1)} %fusion.44), channel_id=1, replica_groups=mesh['leaf'=4,'ctx'=8] {'ctx'}, dimensions={0}, use_global_device_ids=true | all-gather | bytes 108 | tf_op jit(solution)/shard_map/all_gather | solution.py:14
  150.0 1.8 reshape.480
  151.8 1.8 reshape.478
  153.5 1.8 reshape.476
  155.3 1.7 fusion.12
  157.8 1.7 fusion.11
  160.4 1.7 fusion.10
  162.9 1.7 fusion.9
  165.5 2.3 pad_maximum_fusion.1
  168.9 135.4 %all-gather.10.cloned.1.call-done = f32[24,2,128,512]{3,2,1,0:T(8,128)} async-done(((f32[3,2,128,512]{3,2,1,0:T(8,128)}), f32[24,2,128,512]{3,2,1,0:T(8,128)}) %all-gather.10.cloned.1.call-update) | async-done | bytes 12582928 | tf_op jit(solution)/shard_map/all_gather | solution.py:14
  304.3 16.8 %while.22 = (s32[]{:T(128)}, f32[3,2,128,512]{3,2,1,0:T(8,128)S(1)}, s32[]{:T(128)}, f32[8,3]{1,0:T(8,128)S(1)}, f32[8,3,2,128,512]{4,3,2,1,0:T(8,128)}, /*index=5*/s32[]{:T(128)}, s32[]{:T(128)}, s32[]{:T(128)}, s32[]{:T(128)}) while((s32[]{:T(128)}, f32[3,2,128,512]{3,2,1,0:T(8,128)S(1)}, s32[]{:T(128)}, ...), condition=%wide.region_20.21_spmd.clone, body=%wide.region_19.20_spmd.clone.sunk | while | flops 1572875 | bytes 4718785 | solution.py:25
  304.3 2.0 fusion.77
  306.4 2.1 fusion.77
  308.5 2.1 fusion.77
  310.6 2.1 fusion.77
  312.8 2.1 fusion.77
  314.9 2.1 fusion.77
  317.0 2.1 fusion.77
  319.1 2.1 fusion.77
  (155 shorter events, 38.9 us)
Async XLA Ops:
  7.2 11.1 %copy-start.20 = (bf16[128,4096]{1,0:T(8,128)(2,1)S(1)}, bf16[128,4096]{1,0:T(8,128)(2,1)}, u32[]{:S(2)}) copy-start(bf16[128,4096]{1,0:T(8,128)(2,1)} %param.26) | copy-start | bytes 3145732
  7.2 46.0 %all-gather.6.cloned.1.call-start = ((), (), s32[]{:S(2)}) async-start(), calls=%async_computation | async-start | bytes 1179648 | tf_op jit(solution)/shard_map/all_gather | solution.py:98
  7.9 86.4 %all-gather.8.cloned.1.call-start = ((), (), s32[]{:S(2)}) async-start(), calls=%async_computation.1 | async-start | bytes 1179648 | tf_op jit(solution)/shard_map/all_gather | solution.py:99
  8.7 295.7 %all-gather.10.cloned.1.call-start = ((), (), s32[]{:S(2)}) async-start(), calls=%async_computation.2 | async-start | bytes 14155776 | tf_op jit(solution)/shard_map/all_gather | solution.py:14
  18.2 4.4 %copy-start.27 = (s32[128]{0:T(128)S(1)}, s32[128]{0:T(128)}, u32[]{:S(2)}) copy-start(s32[128]{0:T(128)} %param.31) | copy-start | bytes 1540
  18.2 4.4 %copy-start.19 = (bf16[128,4096]{1,0:T(8,128)(2,1)S(1)}, bf16[128,4096]{1,0:T(8,128)(2,1)}, u32[]{:S(2)}) copy-start(bf16[128,4096]{1,0:T(8,128)(2,1)} %param.29) | copy-start | bytes 3145732
  20.1 79.8 %copy-start.12 = (bf16[1024,128]{1,0:T(8,128)(2,1)}, bf16[1024,128]{1,0:T(8,128)(2,1)S(1)}, u32[]{:S(2)}) copy-start(bf16[1024,128]{1,0:T(8,128)(2,1)S(1)} %reshape.481) | copy-start | bytes 786436
  100.0 4.5 %copy-start.5 = (bf16[512,512]{1,0:T(8,128)(2,1)}, bf16[512,512]{1,0:T(8,128)(2,1)S(1)}, u32[]{:S(2)}) copy-start(bf16[512,512]{1,0:T(8,128)(2,1)S(1)} %constant_dynamic-update-slice_fusion) | copy-start | bytes 1572868
  101.6 4.9 %copy-start.7 = (bf16[1024,128]{1,0:T(8,128)(2,1)}, bf16[1024,128]{1,0:T(8,128)(2,1)S(1)}, u32[]{:S(2)}) copy-start(bf16[1024,128]{1,0:T(8,128)(2,1)S(1)} %convolution_convert_fusion) | copy-start | bytes 786436
  103.1 4.7 %copy-start.9 = (bf16[1024,128]{1,0:T(8,128)(2,1)}, bf16[1024,128]{1,0:T(8,128)(2,1)S(1)}, u32[]{:S(2)}) copy-start(bf16[1024,128]{1,0:T(8,128)(2,1)S(1)} %convolution_convert_fusion.1) | copy-start | bytes 786436
  104.5 4.5 %copy-start.10 = (bf16[1024,128]{1,0:T(8,128)(2,1)}, bf16[1024,128]{1,0:T(8,128)(2,1)S(1)}, u32[]{:S(2)}) copy-start(bf16[1024,128]{1,0:T(8,128)(2,1)S(1)} %convolution_convert_fusion.2) | copy-start | bytes 786436
  105.9 5.3 %copy-start.11 = (bf16[1024,128]{1,0:T(8,128)(2,1)}, bf16[1024,128]{1,0:T(8,128)(2,1)S(1)}, u32[]{:S(2)}) copy-start(bf16[1024,128]{1,0:T(8,128)(2,1)S(1)} %convolution_convert_fusion.3) | copy-start | bytes 786436
  107.2 8.4 %copy-start.1 = (bf16[1024,512]{0,1:T(8,128)(2,1)}, bf16[1024,512]{0,1:T(8,128)(2,1)S(1)}, u32[]{:S(2)}) copy-start(bf16[1024,512]{0,1:T(8,128)(2,1)S(1)} %multiply_convert_fusion) | copy-start | bytes 3145732
  108.5 7.7 %copy-start.2 = (bf16[1024,512]{0,1:T(8,128)(2,1)}, bf16[1024,512]{0,1:T(8,128)(2,1)S(1)}, u32[]{:S(2)}) copy-start(bf16[1024,512]{0,1:T(8,128)(2,1)S(1)} %multiply_convert_fusion.1) | copy-start | bytes 3145732
  113.0 2.6 copy-start.13
  115.6 2.2 copy-start.3
  115.6 2.7 copy-start.4
  115.6 2.7 copy-start.18
  119.3 29.8 %copy-start.8 = (bf16[1024,128]{1,0:T(8,128)(2,1)S(1)}, bf16[1024,128]{1,0:T(8,128)(2,1)}, u32[]{:S(2)}) copy-start(bf16[1024,128]{1,0:T(8,128)(2,1)} %copy-done.7) | copy-start | bytes 786436
  120.6 34.7 %copy-start.6 = (bf16[512,512]{1,0:T(8,128)(2,1)S(1)}, bf16[512,512]{1,0:T(8,128)(2,1)}, u32[]{:S(2)}) copy-start(bf16[512,512]{1,0:T(8,128)(2,1)} %copy-done.5) | copy-start | bytes 1572868
  164.6 3.2 copy-start.21
  164.7 3.2 copy-start.22
  165.5 2.3 copy-start.23
  165.5 2.3 copy-start.24
  (7 other events, 8.6 us)
Sparse Core Ops, SparseCore 0:
  10.1 43.0 all-gather.5
  55.3 38.9 all-gather.7
  120.7 183.5 all-gather.9
where the time goes:
time: 331 us; the launch traced here: 330 us
  waiting for transfers between devices  208 us (63%)
  other arithmetic  26.8 us (8%)
  local copies, waits for them, and re-layouts  25.5 us (8%)
  blocking collectives  24.4 us (7%)
  between operations  24.2 us (7%)
  matrix products  20.2 us (6%)
    all_gather x1, waiting for transfers between devices, prefix(): everything = jax.tree.map(lambda part: lax.all_gather(part, axis), x)  135 us
    all_gather x1, waiting for transfers between devices, on_device(): value_piece = lax.all_gather(values, 'ctx', axis=0, tiled=True)  41.1 us
    all_gather x1, waiting for transfers between devices, on_device(): key_piece = lax.all_gather(keys, 'ctx', axis=0, tiled=True)  29.8 us
    all_gather x1, blocking collectives, prefix(): everything = jax.tree.map(lambda part: lax.all_gather(part, axis), x)  24.4 us
    select_n x8, other arithmetic, hop(): return jax.tree.map(lambda a, b: jnp.where(reached, a, b), new, before)  16.4 us
    dot_general x4, matrix products, attend_block(): jnp.dot(grad_score, key_cols, preferred_element_type=jnp.float32) * scaling  6.85 us
  transfers between devices with their start and end apart: 3, of which 3 were waited for; matrix products, arithmetic and copies ran while one was open for 9% of the time, Pallas kernels for 0%

commit v1 on v0

--- a/solution.py
+++ b/solution.py
@@ -7,6 +7,16 @@
 KEY_HEADS = 4
 HEAD_WIDTH = 128
 HEADS_PER_KEY = 8
+
+
+def gather_by_hops(array, name, along):
+    size = lax.axis_size(name)
+    current, blocks = (array, [array])
+    for _ in range(size - 1):
+        current = lax.ppermute(current, name, [(i, (i + 1) % size) for i in range(size)])
+        blocks.insert(0, current)
+    merged = jnp.concatenate(blocks, axis=along)
+    return jnp.roll(merged, (lax.axis_index(name) + 1) * array.shape[along], axis=along)
 
 
 def prefix(x, axis, combine, identity):
@@ -95,7 +105,7 @@
     row_ids = jnp.arange(block_rows, dtype=jnp.int32)
     empty = jnp.zeros((3, block_rows, kv_width), jnp.bfloat16)
     picked = (empty, empty)
-    key_piece = lax.all_gather(keys, "ctx", axis=0, tiled=True)
+    key_piece = gather_by_hops(keys, "ctx", 0)
     value_piece = lax.all_gather(values, "ctx", axis=0, tiled=True)
     piece_rows = key_piece.shape[0]
     for slot_number in range(3):

time: 331 us -> 309 us (0.934)
  waiting for transfers between devices: 208 us -> 176 us
  local copies, waits for them, and re-layouts: 25.5 us -> 32.4 us
  blocking collectives: 24.4 us -> 19.5 us
    all_gather x1, waiting for transfers between devices: 41.1 us -> 0.02 us  [on_device(): value_piece = lax.all_gather(values, 'ctx', axis=0, tiled=True)]
    ppermute x0 -> x7, waiting for transfers between devices: none -> 38.6 us  [gather_by_hops(): lax.ppermute(current, name, [(i, (i + 1) % size) for i in range(size)])]
    all_gather x1 -> x0, waiting for transfers between devices: 29.8 us -> none  [on_device(): key_piece = lax.all_gather(keys, 'ctx', axis=0, tiled=True)]
    unnamed x57 -> x86, local copies, waits for them, and re-layouts: 1.2 us -> 8.68 us
    all_gather x1, blocking collectives: 24.4 us -> 19.5 us  [prefix(): everything = jax.tree.map(lambda part: lax.all_gather(part, axis), x)]
  transfers between devices with their start and end apart: 3 -> 9, of which waited for: 3 -> 8; matrix products, arithmetic and copies ran while one was open for 9% -> 12% of each run, Pallas kernels for 0% -> 0%
where the time goes in v1:
time: 309 us; the launch traced here: 307 us
  waiting for transfers between devices  176 us (57%)
  local copies, waits for them, and re-layouts  32.4 us (10%)
  other arithmetic  28.7 us (9%)
  between operations  24.3 us (8%)
  matrix products  22.4 us (7%)
  blocking collectives  19.5 us (6%)
  starting transfers between devices  3.25 us (1%)
    all_gather x1, waiting for transfers between devices, prefix(): everything = jax.tree.map(lambda part: lax.all_gather(part, axis), x)  137 us
    ppermute x7, waiting for transfers between devices, gather_by_hops(): lax.ppermute(current, name, [(i, (i + 1) % size) for i in range(size)])  38.6 us
    all_gather x1, blocking collectives, prefix(): everything = jax.tree.map(lambda part: lax.all_gather(part, axis), x)  19.5 us
    select_n x8, other arithmetic, hop(): return jax.tree.map(lambda a, b: jnp.where(reached, a, b), new, before)  16.4 us
    unnamed x86, local copies, waits for them, and re-layouts  8.68 us
    dot_general x8, matrix products, dot_rows(): lax.dot_general(left, right, (((1,), (1,)), ((), ())), preferred_element_...  8.21 us
    dot_general x4, matrix products, attend_block(): jnp.dot(grad_score, key_cols, preferred_element_type=jnp.float32) * scaling  6.86 us
  transfers between devices with their start and end apart: 9, of which 8 were waited for; matrix products, arithmetic and copies ran while one was open for 12% of the time, Pallas kernels for 0%

profile of v1, /device:TPU:0, one launch (start us, length us, event | category | flops | bytes accessed | tf_op | source)
XLA Modules:
  0.0 307.2 jit_solution(5131490607370535341)
XLA Ops:
  7.2 3.0 collective-permute-start
  17.3 7.5 %collective-permute-done.1 = bf16[128,512]{1,0:T(8,128)(2,1)S(1)} collective-permute-done((bf16[128,512]{1,0:T(8,128)(2,1)S(1)}, bf16[128,512]{1,0:T(8,128)(2,1)S(1)}, u32[]{:S(2)}, u32[]{:S(2)}) %collective-permute-start.1) | collective-permute-done | bytes 131104 | tf_op jit(solution)/shard_map/ppermute | solution.py:16
  29.3 4.0 %collective-permute-done.2 = bf16[128,512]{1,0:T(8,128)(2,1)S(1)} collective-permute-done((bf16[128,512]{1,0:T(8,128)(2,1)S(1)}, bf16[128,512]{1,0:T(8,128)(2,1)S(1)}, u32[]{:S(2)}, u32[]{:S(2)}) %collective-permute-start.2) | collective-permute-done | bytes 131104 | tf_op jit(solution)/shard_map/ppermute | solution.py:16
  33.4 7.7 %collective-permute-done.3 = bf16[128,512]{1,0:T(8,128)(2,1)S(1)} collective-permute-done((bf16[128,512]{1,0:T(8,128)(2,1)S(1)}, bf16[128,512]{1,0:T(8,128)(2,1)S(1)}, u32[]{:S(2)}, u32[]{:S(2)}) %collective-permute-start.3) | collective-permute-done | bytes 131104 | tf_op jit(solution)/shard_map/ppermute | solution.py:16
  41.9 7.6 %collective-permute-done.4 = bf16[128,512]{1,0:T(8,128)(2,1)} collective-permute-done((bf16[128,512]{1,0:T(8,128)(2,1)S(1)}, bf16[128,512]{1,0:T(8,128)(2,1)}, u32[]{:S(2)}, u32[]{:S(2)}) %collective-permute-start.4) | collective-permute-done | bytes 131104 | tf_op jit(solution)/shard_map/ppermute | solution.py:16
  50.3 1.8 reshape.481
  54.6 3.7 %collective-permute-done.5 = bf16[128,512]{1,0:T(8,128)(2,1)} collective-permute-done((bf16[128,512]{1,0:T(8,128)(2,1)}, bf16[128,512]{1,0:T(8,128)(2,1)}, u32[]{:S(2)}, u32[]{:S(2)}) %collective-permute-start.5) | collective-permute-done | bytes 131104 | tf_op jit(solution)/shard_map/ppermute | solution.py:16
  59.6 6.6 %collective-permute-done.6 = bf16[128,512]{1,0:T(8,128)(2,1)} collective-permute-done((bf16[128,512]{1,0:T(8,128)(2,1)}, bf16[128,512]{1,0:T(8,128)(2,1)}, u32[]{:S(2)}, u32[]{:S(2)}) %collective-permute-start.6) | collective-permute-done | bytes 131104 | tf_op jit(solution)/shard_map/ppermute | solution.py:16
  73.0 3.3 %conditional.3 = (bf16[3,128,512]{2,1,0:T(8,128)(2,1)S(1)}, bf16[3,128,512]{2,1,0:T(8,128)(2,1)S(1)}) conditional(s32[]{:T(128)} %convert_element_type.109, () %tuple.88, (s32[]{:T(128)}, s32[128]{0:T(128)S(1)}, bf16[1024,512]{1,0:T(8,128)(2,1)S(1)}, bf16[1024,512]{1,0:T(8,128)(2,1)}) %tuple.89), branch_computations={%region_1.2_spmd, %region_2.3_spmd} | conditional | flops 133248 | bytes 2104604 | solution.py:130
  73.1 2.2 gather_fusion.1
  103.2 19.5 %all-gather.1 = f32[8,1,3]{2,1,0:T(1,128)S(1)} all-gather(f32[1,1,3]{2,1,0:T(1,128)S(1)} %fusion.44), channel_id=1, replica_groups=mesh['leaf'=4,'ctx'=8] {'ctx'}, dimensions={0}, use_global_device_ids=true | all-gather | bytes 108 | tf_op jit(solution)/shard_map/all_gather | solution.py:24
  127.1 1.8 reshape.478
  128.8 1.8 reshape.476
  140.8 2.3 pad_maximum_fusion.1
  144.2 137.4 %all-gather.7.cloned.1.call-done = f32[24,2,128,512]{3,2,1,0:T(8,128)} async-done(((f32[3,2,128,512]{3,2,1,0:T(8,128)}), f32[24,2,128,512]{3,2,1,0:T(8,128)}) %all-gather.7.cloned.1.call-update) | async-done | bytes 12582928 | tf_op jit(solution)/shard_map/all_gather | solution.py:24
  281.6 16.8 %while.22 = (s32[]{:T(128)}, f32[3,2,128,512]{3,2,1,0:T(8,128)S(1)}, s32[]{:T(128)}, f32[8,3]{1,0:T(8,128)S(1)}, f32[8,3,2,128,512]{4,3,2,1,0:T(8,128)}, /*index=5*/s32[]{:T(128)}, s32[]{:T(128)}, s32[]{:T(128)}, s32[]{:T(128)}) while((s32[]{:T(128)}, f32[3,2,128,512]{3,2,1,0:T(8,128)S(1)}, s32[]{:T(128)}, ...), condition=%wide.region_20.21_spmd.clone, body=%wide.region_19.20_spmd.clone.sunk | while | flops 1572875 | bytes 4718785 | solution.py:35
  281.6 2.0 fusion.77
  283.7 2.1 fusion.77
  285.8 2.1 fusion.77
  287.9 2.1 fusion.77
  290.0 2.1 fusion.77
  292.1 2.1 fusion.77
  294.2 2.1 fusion.77
  296.3 2.1 fusion.77
  (197 shorter events, 59.1 us)
Async XLA Ops:
  7.2 10.0 %copy-start.34 = (s32[8,4]{0,1:T(4,128)S(1)}, s32[8,4]{0,1:T(4,128)}, u32[]{:S(2)}) copy-start(s32[8,4]{0,1:T(4,128)} %param.30) | copy-start | bytes 388
  7.2 42.4 %copy-start.22 = (bf16[128,4096]{1,0:T(8,128)(2,1)S(1)}, bf16[128,4096]{1,0:T(8,128)(2,1)}, u32[]{:S(2)}) copy-start(bf16[128,4096]{1,0:T(8,128)(2,1)} %param.26) | copy-start | bytes 3145732
  7.2 65.8 %all-gather.5.cloned.1.call-start = ((), (), s32[]{:S(2)}) async-start(), calls=%async_computation | async-start | bytes 1179648 | tf_op jit(solution)/shard_map/all_gather | solution.py:109
  7.2 9.8 %collective-permute-start = (bf16[128,512]{1,0:T(8,128)(2,1)}, bf16[128,512]{1,0:T(8,128)(2,1)S(1)}, u32[]{:S(2)}, u32[]{:S(2)}) collective-permute-start(bf16[128,512]{1,0:T(8,128)(2,1)} %param.27), channel_id=1, source_target_pairs={{0,1},{1,2},{2,3},{3,4},{4,5},{5,6},{6,7},{7,0},{8,9},{9,10},{10,1... | collective-permute-start | bytes 393224 | tf_op jit(solution)/shard_map/ppermute | solution.py:16
  10.3 271.3 %all-gather.7.cloned.1.call-start = ((), (), s32[]{:S(2)}) async-start(), calls=%async_computation.1 | async-start | bytes 14155776 | tf_op jit(solution)/shard_map/all_gather | solution.py:24
  17.0 7.8 %collective-permute-start.1 = (bf16[128,512]{1,0:T(8,128)(2,1)S(1)}, bf16[128,512]{1,0:T(8,128)(2,1)S(1)}, u32[]{:S(2)}, u32[]{:S(2)}) collective-permute-start(bf16[128,512]{1,0:T(8,128)(2,1)S(1)} %collective-permute-done), channel_id=1, source_target_pairs={{0,1},{1,2},{2,3},{3,4},{4,5},{5,6},{6,7},{7,0},{8,9},{9,10},{10,1... | collective-permute-start | bytes 393224 | tf_op jit(solution)/shard_map/ppermute | solution.py:16
  24.8 16.3 %copy-start.28 = (bf16[128,512]{1,0:T(8,128)(2,1)}, bf16[128,512]{1,0:T(8,128)(2,1)S(1)}, u32[]{:S(2)}) copy-start(bf16[128,512]{1,0:T(8,128)(2,1)S(1)} %collective-permute-done.1) | copy-start | bytes 393220
  24.8 8.5 %collective-permute-start.2 = (bf16[128,512]{1,0:T(8,128)(2,1)S(1)}, bf16[128,512]{1,0:T(8,128)(2,1)S(1)}, u32[]{:S(2)}, u32[]{:S(2)}) collective-permute-start(bf16[128,512]{1,0:T(8,128)(2,1)S(1)} %collective-permute-done.1), channel_id=1, source_target_pairs={{0,1},{1,2},{2,3},{3,4},{4,5},{5,6},{6,7},{7,0},{8,9},{9,10},{10,1... | collective-permute-start | bytes 393224 | tf_op jit(solution)/shard_map/ppermute | solution.py:16
  33.3 7.7 %copy-start.30 = (bf16[128,512]{1,0:T(8,128)(2,1)}, bf16[128,512]{1,0:T(8,128)(2,1)S(1)}, u32[]{:S(2)}) copy-start(bf16[128,512]{1,0:T(8,128)(2,1)S(1)} %collective-permute-done.2) | copy-start | bytes 393220
  33.3 7.7 %collective-permute-start.3 = (bf16[128,512]{1,0:T(8,128)(2,1)S(1)}, bf16[128,512]{1,0:T(8,128)(2,1)S(1)}, u32[]{:S(2)}, u32[]{:S(2)}) collective-permute-start(bf16[128,512]{1,0:T(8,128)(2,1)S(1)} %collective-permute-done.2), channel_id=1, source_target_pairs={{0,1},{1,2},{2,3},{3,4},{4,5},{5,6},{6,7},{7,0},{8,9},{9,10},{10,1... | collective-permute-start | bytes 393224 | tf_op jit(solution)/shard_map/ppermute | solution.py:16
  41.1 8.5 %copy-start.32 = (bf16[128,512]{1,0:T(8,128)(2,1)}, bf16[128,512]{1,0:T(8,128)(2,1)S(1)}, u32[]{:S(2)}) copy-start(bf16[128,512]{1,0:T(8,128)(2,1)S(1)} %collective-permute-done.3) | copy-start | bytes 393220
  41.1 8.5 %collective-permute-start.4 = (bf16[128,512]{1,0:T(8,128)(2,1)S(1)}, bf16[128,512]{1,0:T(8,128)(2,1)}, u32[]{:S(2)}, u32[]{:S(2)}) collective-permute-start(bf16[128,512]{1,0:T(8,128)(2,1)S(1)} %collective-permute-done.3), channel_id=1, source_target_pairs={{0,1},{1,2},{2,3},{3,4},{4,5},{5,6},{6,7},{7,0},{8,9},{9,10},{10,1... | collective-permute-start | bytes 393224 | tf_op jit(solution)/shard_map/ppermute | solution.py:16
  49.5 8.8 %collective-permute-start.5 = (bf16[128,512]{1,0:T(8,128)(2,1)}, bf16[128,512]{1,0:T(8,128)(2,1)}, u32[]{:S(2)}, u32[]{:S(2)}) collective-permute-start(bf16[128,512]{1,0:T(8,128)(2,1)} %collective-permute-done.4), channel_id=1, source_target_pairs={{0,1},{1,2},{2,3},{3,4},{4,5},{5,6},{6,7},{7,0},{8,9},{9,10},{10,1... | collective-permute-start | bytes 393224 | tf_op jit(solution)/shard_map/ppermute | solution.py:16
  58.3 8.0 %collective-permute-start.6 = (bf16[128,512]{1,0:T(8,128)(2,1)}, bf16[128,512]{1,0:T(8,128)(2,1)}, u32[]{:S(2)}, u32[]{:S(2)}) collective-permute-start(bf16[128,512]{1,0:T(8,128)(2,1)} %collective-permute-done.5), channel_id=1, source_target_pairs={{0,1},{1,2},{2,3},{3,4},{4,5},{5,6},{6,7},{7,0},{8,9},{9,10},{10,1... | collective-permute-start | bytes 393224 | tf_op jit(solution)/shard_map/ppermute | solution.py:16
  58.4 11.6 %copy-start.31 = (bf16[128,512]{1,0:T(8,128)(2,1)S(1)}, bf16[128,512]{1,0:T(8,128)(2,1)}, u32[]{:S(2)}) copy-start(bf16[128,512]{1,0:T(8,128)(2,1)} %copy-done.30) | copy-start | bytes 393220
  58.4 11.6 %copy-start.29 = (bf16[128,512]{1,0:T(8,128)(2,1)S(1)}, bf16[128,512]{1,0:T(8,128)(2,1)}, u32[]{:S(2)}) copy-start(bf16[128,512]{1,0:T(8,128)(2,1)} %copy-done.28) | copy-start | bytes 393220
  58.4 11.6 %copy-start.21 = (bf16[128,512]{1,0:T(8,128)(2,1)S(1)}, bf16[128,512]{1,0:T(8,128)(2,1)}, u32[]{:S(2)}) copy-start(bf16[128,512]{1,0:T(8,128)(2,1)} %param.27) | copy-start | bytes 393220
  58.7 28.5 %copy-start.6 = (bf16[1024,128]{1,0:T(8,128)(2,1)}, bf16[1024,128]{1,0:T(8,128)(2,1)S(1)}, u32[]{:S(2)}) copy-start(bf16[1024,128]{1,0:T(8,128)(2,1)S(1)} %reshape.487) | copy-start | bytes 786436
  58.7 14.1 %copy-start.33 = (bf16[128,512]{1,0:T(8,128)(2,1)S(1)}, bf16[128,512]{1,0:T(8,128)(2,1)}, u32[]{:S(2)}) copy-start(bf16[128,512]{1,0:T(8,128)(2,1)} %copy-done.32) | copy-start | bytes 393220
  85.4 6.3 %copy-start.14 = (bf16[1024,128]{1,0:T(8,128)(2,1)}, bf16[1024,128]{1,0:T(8,128)(2,1)S(1)}, u32[]{:S(2)}) copy-start(bf16[1024,128]{1,0:T(8,128)(2,1)S(1)} %convolution_convert_fusion.3) | copy-start | bytes 786436
  86.7 9.4 %copy-start.1 = (bf16[1024,512]{0,1:T(8,128)(2,1)}, bf16[1024,512]{0,1:T(8,128)(2,1)S(1)}, u32[]{:S(2)}) copy-start(bf16[1024,512]{0,1:T(8,128)(2,1)S(1)} %multiply_convert_fusion) | copy-start | bytes 3145732
  88.9 7.7 %copy-start.2 = (bf16[1024,512]{0,1:T(8,128)(2,1)}, bf16[1024,512]{0,1:T(8,128)(2,1)S(1)}, u32[]{:S(2)}) copy-start(bf16[1024,512]{0,1:T(8,128)(2,1)S(1)} %multiply_convert_fusion.1) | copy-start | bytes 3145732
  99.8 24.7 %copy-start.11 = (bf16[1024,128]{1,0:T(8,128)(2,1)S(1)}, bf16[1024,128]{1,0:T(8,128)(2,1)}, u32[]{:S(2)}) copy-start(bf16[1024,128]{1,0:T(8,128)(2,1)} %copy-done.10) | copy-start | bytes 786436
  101.1 29.5 %copy-start.8 = (bf16[512,512]{1,0:T(8,128)(2,1)S(1)}, bf16[512,512]{1,0:T(8,128)(2,1)}, u32[]{:S(2)}) copy-start(bf16[512,512]{1,0:T(8,128)(2,1)} %copy-done.7) | copy-start | bytes 1572868
  (20 other events, 52.8 us)
Sparse Core Ops, SparseCore 0:
  10.4 44.7 all-gather.4
  101.2 180.3 all-gather.6
